TPU v7x, 16 devices: a 4x2x1 block of a 4x4x8 slice. The times are simulated.
16 devices in a mesh: batch: 2 (over y, z), row: 8 (over x, core).
Axes of the slice: x: 4, y: 2, z: 1, core: 2. Of those that a mesh axis runs over, the one named last changes fastest.
The devices are a block of a 4x4x8 slice.
Arguments:
- trans_mat: bfloat16 [32768, 16384], P(('batch', 'row')), parts along dimension 0
- teleport: float32 [32768, 128], P(('batch', 'row')), parts along dimension 0
- dangling: int32 [32768], P(('batch', 'row')), parts along dimension 0
- damping: float32 [16], replicated
- rank_init: float32 [32768, 128], P(('batch', 'row')), parts along dimension 0
Outputs:
- output: float32 [32768, 128], P(('batch', 'row')), parts along dimension 0
There are 2 independent parts. A program takes and returns all parts, laid end to end along the dimension named above; an argument that names none is the same for every part.
All inputs are finite; a program needn't handle non-finite values.
Results may differ from a plain program's by a relative error of at most 0.001.
Values are sent between devices in bfloat16 or wider.
A program may use at most 768 MiB of HBM per device.

v0:
```python
import jax
import jax.numpy as jnp
from jax import lax
from jax.sharding import PartitionSpec as P, NamedSharding


def solution(mesh):
    spec_rows = P(("batch", "row"), None)
    spec_vec = P(("batch", "row"))

    def local_sweeps(mat_rows, tele_rows, dang_rows, damping, start_rows):
        num_nodes = mat_rows.shape[1]
        dang_float = dang_rows.astype(jnp.float32)
        rank_rows = start_rows
        for sweep_idx in range(damping.shape[0]):
            gathered = lax.all_gather(rank_rows.astype(jnp.bfloat16), "row", axis=0, tiled=True)
            dang_mass = lax.psum(jnp.dot(dang_float, rank_rows, preferred_element_type=jnp.float32), "row")
            prod_rows = jnp.dot(mat_rows, gathered, preferred_element_type=jnp.float32)
            factor = damping[sweep_idx]
            rank_rows = factor * prod_rows + (1.0 - factor) * tele_rows + (factor / num_nodes) * dang_mass[None, :]
        return rank_rows

    sharded_fn = jax.shard_map(local_sweeps, mesh=mesh, in_specs=(spec_rows, spec_rows, spec_vec, P(None), spec_rows), out_specs=spec_rows, check_vma=False)
    return sharded_fn
```

profile of v0, /device:TPU:113, one launch (start us, length us, event | category | flops | bytes accessed | tf_op | source)
XLA Modules:
  0.0 948.3 jit_solution(9041940064169245938)
XLA Ops:
  14.1 14.1 %psum.112 = f32[128]{0:T(128)S(1)} all-reduce(f32[128]{0:T(128)S(1)} %convolution_bitcast_fusion.15), channel_id=1, replica_groups=mesh['batch'=2,'row'=8] {'row'}, use_global_device_ids=true, to_apply=%region_0.0 | all-reduce | flops 128 | bytes 1024 | tf_op jit(solution)/shard_map/psum | solution.py:17
  40.2 29.5 %fusion.16 = bf16[2048,128]{1,0:T(8,128)(2,1)} fusion(bf16[2048,16384]{1,0:T(8,128)(2,1)} %param.5, bf16[16384,128]{1,0:T(8,128)(2,1)} %all-gather.17.cloned.1.call-done, f32[2048,128]{1,0:T(8,128)} %param.6, f32[128]{0:T(128)S(1)} %broadcast_multiply_fusion.15, f32[]{:T(128)S(6)} %sub.48, f32[]{:T(128)} %bitcast.15), kind=kOutput, calls=%fused_computation.32 | convolution fusion | flops 8591245312 | bytes 72876552 | tf_op jit(solution)/shard_map/dot_general | solution.py:18
  72.7 12.7 %psum.113 = f32[128]{0:T(128)S(1)} all-reduce(f32[128]{0:T(128)S(1)} %convolution_bitcast_fusion.14), channel_id=1, replica_groups=mesh['batch'=2,'row'=8] {'row'}, use_global_device_ids=true, to_apply=%region_1.0 | all-reduce | flops 128 | bytes 1024 | tf_op jit(solution)/shard_map/psum | solution.py:17
  97.7 30.5 %fusion.18 = bf16[2048,128]{0,1:T(8,128)(2,1)} fusion(bf16[16384,128]{1,0:T(8,128)(2,1)} %all-gather.19.cloned.1.call-done, bf16[2048,16384]{1,0:T(8,128)(2,1)} %param.5, f32[2048,128]{0,1:T(8,128)S(1)} %copy.6, f32[128]{0:T(128)S(1)} %broadcast_multiply_fusion.14, f32[]{:T(128)S(6)} %sub.49, f32[]{:T(128)} %bitcast.14), kind=kOutput, calls=%fused_computation.34 | convolution fusion | flops 8591245312 | bytes 72876552 | tf_op jit(solution)/shard_map/dot_general | solution.py:18
  130.7 12.6 %psum.114 = f32[128]{0:T(128)S(1)} all-reduce(f32[128]{0:T(128)S(1)} %convolution_bitcast_fusion.13), channel_id=1, replica_groups=mesh['batch'=2,'row'=8] {'row'}, use_global_device_ids=true, to_apply=%region_2.0 | all-reduce | flops 128 | bytes 1024 | tf_op jit(solution)/shard_map/psum | solution.py:17
  143.3 12.7 %all-gather.21.cloned.1.call-done = bf16[16384,128]{0,1:T(8,128)(2,1)} async-done(((bf16[2048,128]{0,1:T(8,128)(2,1)}), bf16[16384,128]{0,1:T(8,128)(2,1)}) %all-gather.21.cloned.1.call-update) | async-done | bytes 4194320 | tf_op jit(solution)/shard_map/all_gather | solution.py:16
  156.1 30.0 %fusion.20 = bf16[2048,128]{0,1:T(8,128)(2,1)} fusion(bf16[16384,128]{0,1:T(8,128)(2,1)} %all-gather.21.cloned.1.call-done, bf16[2048,16384]{1,0:T(8,128)(2,1)} %param.5, f32[2048,128]{0,1:T(8,128)S(1)} %copy.6, f32[128]{0:T(128)S(1)} %broadcast_multiply_fusion.13, f32[]{:T(128)S(6)} %sub.50, f32[]{:T(128)} %bitcast.13), kind=kOutput, calls=%fused_computation.36 | convolution fusion | flops 8591245312 | bytes 72876552 | tf_op jit(solution)/shard_map/dot_general | solution.py:18
  188.6 12.8 %psum.115 = f32[128]{0:T(128)S(1)} all-reduce(f32[128]{0:T(128)S(1)} %convolution_bitcast_fusion.12), channel_id=1, replica_groups=mesh['batch'=2,'row'=8] {'row'}, use_global_device_ids=true, to_apply=%region_3.0 | all-reduce | flops 128 | bytes 1024 | tf_op jit(solution)/shard_map/psum | solution.py:17
  214.0 30.0 %fusion.22 = bf16[2048,128]{0,1:T(8,128)(2,1)} fusion(bf16[16384,128]{0,1:T(8,128)(2,1)} %all-gather.23.cloned.1.call-done, bf16[2048,16384]{1,0:T(8,128)(2,1)} %param.5, f32[2048,128]{0,1:T(8,128)S(1)} %copy.6, f32[128]{0:T(128)S(1)} %broadcast_multiply_fusion.12, f32[]{:T(128)S(6)} %sub.51, f32[]{:T(128)} %bitcast.12), kind=kOutput, calls=%fused_computation.38 | convolution fusion | flops 8591245312 | bytes 72876552 | tf_op jit(solution)/shard_map/dot_general | solution.py:18
  246.8 12.6 %psum.116 = f32[128]{0:T(128)S(1)} all-reduce(f32[128]{0:T(128)S(1)} %convolution_bitcast_fusion.11), channel_id=1, replica_groups=mesh['batch'=2,'row'=8] {'row'}, use_global_device_ids=true, to_apply=%region_4.0 | all-reduce | flops 128 | bytes 1024 | tf_op jit(solution)/shard_map/psum | solution.py:17
  271.9 30.1 %fusion.24 = bf16[2048,128]{0,1:T(8,128)(2,1)} fusion(bf16[16384,128]{0,1:T(8,128)(2,1)} %all-gather.25.cloned.1.call-done, bf16[2048,16384]{1,0:T(8,128)(2,1)} %param.5, f32[2048,128]{0,1:T(8,128)S(1)} %copy.6, f32[128]{0:T(128)S(1)} %broadcast_multiply_fusion.11, f32[]{:T(128)S(6)} %sub.52, f32[]{:T(128)} %bitcast.11), kind=kOutput, calls=%fused_computation.40 | convolution fusion | flops 8591245312 | bytes 72876552 | tf_op jit(solution)/shard_map/dot_general | solution.py:18
  330.0 30.1 %fusion.26 = bf16[2048,128]{0,1:T(8,128)(2,1)} fusion(bf16[16384,128]{0,1:T(8,128)(2,1)} %all-gather.27.cloned.1.call-done, bf16[2048,16384]{1,0:T(8,128)(2,1)} %param.5, f32[2048,128]{0,1:T(8,128)S(1)} %copy.6, f32[128]{0:T(128)S(1)} %broadcast_multiply_fusion.10, f32[]{:T(128)S(6)} %sub.53, f32[]{:T(128)} %bitcast.10), kind=kOutput, calls=%fused_computation.42 | convolution fusion | flops 8591245312 | bytes 72876552 | tf_op jit(solution)/shard_map/dot_general | solution.py:18
  375.3 12.7 %all-gather.29.cloned.1.call-done = bf16[16384,128]{0,1:T(8,128)(2,1)} async-done(((bf16[2048,128]{0,1:T(8,128)(2,1)}), bf16[16384,128]{0,1:T(8,128)(2,1)}) %all-gather.29.cloned.1.call-update) | async-done | bytes 4194320 | tf_op jit(solution)/shard_map/all_gather | solution.py:16
  388.0 30.0 %fusion.28 = bf16[2048,128]{0,1:T(8,128)(2,1)} fusion(bf16[16384,128]{0,1:T(8,128)(2,1)} %all-gather.29.cloned.1.call-done, bf16[2048,16384]{1,0:T(8,128)(2,1)} %param.5, f32[2048,128]{0,1:T(8,128)S(1)} %copy.6, f32[128]{0:T(128)S(1)} %broadcast_multiply_fusion.9, f32[]{:T(128)S(6)} %sub.54, f32[]{:T(128)} %bitcast.9), kind=kOutput, calls=%fused_computation.44 | convolution fusion | flops 8591245312 | bytes 72876552 | tf_op jit(solution)/shard_map/dot_general | solution.py:18
  420.8 12.9 %psum.119 = f32[128]{0:T(128)S(1)} all-reduce(f32[128]{0:T(128)S(1)} %convolution_bitcast_fusion.8), channel_id=1, replica_groups=mesh['batch'=2,'row'=8] {'row'}, use_global_device_ids=true, to_apply=%region_7.0 | all-reduce | flops 128 | bytes 1024 | tf_op jit(solution)/shard_map/psum | solution.py:17
  445.9 30.1 %fusion.30 = bf16[2048,128]{0,1:T(8,128)(2,1)} fusion(bf16[16384,128]{0,1:T(8,128)(2,1)} %all-gather.31.cloned.1.call-done, bf16[2048,16384]{1,0:T(8,128)(2,1)} %param.5, f32[2048,128]{0,1:T(8,128)S(1)} %copy.6, f32[128]{0:T(128)S(1)} %broadcast_multiply_fusion.8, f32[]{:T(128)S(6)} %sub.55, f32[]{:T(128)} %bitcast.8), kind=kOutput, calls=%fused_computation.46 | convolution fusion | flops 8591245312 | bytes 72876552 | tf_op jit(solution)/shard_map/dot_general | solution.py:18
  491.3 12.8 %all-gather.33.cloned.1.call-done = bf16[16384,128]{0,1:T(8,128)(2,1)} async-done(((bf16[2048,128]{0,1:T(8,128)(2,1)}), bf16[16384,128]{0,1:T(8,128)(2,1)}) %all-gather.33.cloned.1.call-update) | async-done | bytes 4194320 | tf_op jit(solution)/shard_map/all_gather | solution.py:16
  504.0 30.0 %fusion.32 = bf16[2048,128]{0,1:T(8,128)(2,1)} fusion(bf16[16384,128]{0,1:T(8,128)(2,1)} %all-gather.33.cloned.1.call-done, bf16[2048,16384]{1,0:T(8,128)(2,1)} %param.5, f32[2048,128]{0,1:T(8,128)S(1)} %copy.6, f32[128]{0:T(128)S(1)} %broadcast_multiply_fusion.7, f32[]{:T(128)S(6)} %sub.56, f32[]{:T(128)} %bitcast.7), kind=kOutput, calls=%fused_computation.48 | convolution fusion | flops 8591245312 | bytes 72876552 | tf_op jit(solution)/shard_map/dot_general | solution.py:18
  536.7 12.7 %psum.121 = f32[128]{0:T(128)S(1)} all-reduce(f32[128]{0:T(128)S(1)} %convolution_bitcast_fusion.6), channel_id=1, replica_groups=mesh['batch'=2,'row'=8] {'row'}, use_global_device_ids=true, to_apply=%region_9.0 | all-reduce | flops 128 | bytes 1024 | tf_op jit(solution)/shard_map/psum | solution.py:17
  562.0 30.1 %fusion.34 = bf16[2048,128]{0,1:T(8,128)(2,1)} fusion(bf16[16384,128]{0,1:T(8,128)(2,1)} %all-gather.35.cloned.1.call-done, bf16[2048,16384]{1,0:T(8,128)(2,1)} %param.5, f32[2048,128]{0,1:T(8,128)S(1)} %copy.6, f32[128]{0:T(128)S(1)} %broadcast_multiply_fusion.6, f32[]{:T(128)S(6)} %sub.57, f32[]{:T(128)} %bitcast.6), kind=kOutput, calls=%fused_computation.50 | convolution fusion | flops 8591245312 | bytes 72876552 | tf_op jit(solution)/shard_map/dot_general | solution.py:18
  594.6 12.6 %psum.122 = f32[128]{0:T(128)S(1)} all-reduce(f32[128]{0:T(128)S(1)} %convolution_bitcast_fusion.5), channel_id=1, replica_groups=mesh['batch'=2,'row'=8] {'row'}, use_global_device_ids=true, to_apply=%region_10.0 | all-reduce | flops 128 | bytes 1024 | tf_op jit(solution)/shard_map/psum | solution.py:17
  619.9 30.1 %fusion.36 = bf16[2048,128]{0,1:T(8,128)(2,1)} fusion(bf16[16384,128]{0,1:T(8,128)(2,1)} %all-gather.37.cloned.1.call-done, bf16[2048,16384]{1,0:T(8,128)(2,1)} %param.5, f32[2048,128]{0,1:T(8,128)S(1)} %copy.6, f32[128]{0:T(128)S(1)} %broadcast_multiply_fusion.5, f32[]{:T(128)S(6)} %sub.58, f32[]{:T(128)} %bitcast.5), kind=kOutput, calls=%fused_computation.52 | convolution fusion | flops 8591245312 | bytes 72876552 | tf_op jit(solution)/shard_map/dot_general | solution.py:18
  652.6 12.9 %psum.123 = f32[128]{0:T(128)S(1)} all-reduce(f32[128]{0:T(128)S(1)} %convolution_bitcast_fusion.4), channel_id=1, replica_groups=mesh['batch'=2,'row'=8] {'row'}, use_global_device_ids=true, to_apply=%region_11.0 | all-reduce | flops 128 | bytes 1024 | tf_op jit(solution)/shard_map/psum | solution.py:17
  677.9 30.1 %fusion.38 = bf16[2048,128]{0,1:T(8,128)(2,1)} fusion(bf16[16384,128]{0,1:T(8,128)(2,1)} %all-gather.39.cloned.1.call-done, bf16[2048,16384]{1,0:T(8,128)(2,1)} %param.5, f32[2048,128]{0,1:T(8,128)S(1)} %copy.6, f32[128]{0:T(128)S(1)} %broadcast_multiply_fusion.4, f32[]{:T(128)S(6)} %sub.59, f32[]{:T(128)} %bitcast.4), kind=kOutput, calls=%fused_computation.54 | convolution fusion | flops 8591245312 | bytes 72876552 | tf_op jit(solution)/shard_map/dot_general | solution.py:18
  723.3 12.7 %all-gather.41.cloned.1.call-done = bf16[16384,128]{0,1:T(8,128)(2,1)} async-done(((bf16[2048,128]{0,1:T(8,128)(2,1)}), bf16[16384,128]{0,1:T(8,128)(2,1)}) %all-gather.41.cloned.1.call-update) | async-done | bytes 4194320 | tf_op jit(solution)/shard_map/all_gather | solution.py:16
  735.9 30.1 %fusion.40 = bf16[2048,128]{0,1:T(8,128)(2,1)} fusion(bf16[16384,128]{0,1:T(8,128)(2,1)} %all-gather.41.cloned.1.call-done, bf16[2048,16384]{1,0:T(8,128)(2,1)} %param.5, f32[2048,128]{0,1:T(8,128)S(1)} %copy.6, f32[128]{0:T(128)S(1)} %broadcast_multiply_fusion.3, f32[]{:T(128)S(6)} %sub.60, f32[]{:T(128)} %bitcast.3), kind=kOutput, calls=%fused_computation.56 | convolution fusion | flops 8591245312 | bytes 72876552 | tf_op jit(solution)/shard_map/dot_general | solution.py:18
  793.9 30.1 %fusion.42 = bf16[2048,128]{0,1:T(8,128)(2,1)} fusion(bf16[16384,128]{0,1:T(8,128)(2,1)} %all-gather.43.cloned.1.call-done, bf16[2048,16384]{1,0:T(8,128)(2,1)} %param.5, f32[2048,128]{0,1:T(8,128)S(1)} %copy.6, f32[128]{0:T(128)S(1)} %broadcast_multiply_fusion.2, f32[]{:T(128)S(6)} %sub.61, f32[]{:T(128)} %bitcast.2), kind=kOutput, calls=%fused_computation.58 | convolution fusion | flops 8591245312 | bytes 72876552 | tf_op jit(solution)/shard_map/dot_general | solution.py:18
  839.2 12.7 %all-gather.45.cloned.1.call-done = bf16[16384,128]{0,1:T(8,128)(2,1)} async-done(((bf16[2048,128]{0,1:T(8,128)(2,1)}), bf16[16384,128]{0,1:T(8,128)(2,1)}) %all-gather.45.cloned.1.call-update) | async-done | bytes 4194320 | tf_op jit(solution)/shard_map/all_gather | solution.py:16
  851.9 30.0 %fusion.44 = bf16[2048,128]{0,1:T(8,128)(2,1)} fusion(bf16[16384,128]{0,1:T(8,128)(2,1)} %all-gather.45.cloned.1.call-done, bf16[2048,16384]{1,0:T(8,128)(2,1)} %param.5, f32[2048,128]{0,1:T(8,128)S(1)} %copy.6, f32[128]{0:T(128)S(1)} %broadcast_multiply_fusion.1, f32[]{:T(128)S(6)} %sub.62, f32[]{:T(128)} %bitcast.1), kind=kOutput, calls=%fused_computation.60 | convolution fusion | flops 8591245312 | bytes 72876552 | tf_op jit(solution)/shard_map/dot_general | solution.py:18
  884.4 12.6 %psum.127 = f32[128]{0:T(128)S(1)} all-reduce(f32[128]{0:T(128)S(1)} %convolution_bitcast_fusion), channel_id=1, replica_groups=mesh['batch'=2,'row'=8] {'row'}, use_global_device_ids=true, to_apply=%region_15.0 | all-reduce | flops 128 | bytes 1024 | tf_op jit(solution)/shard_map/psum | solution.py:17
  897.1 12.8 %all-gather.47.cloned.1.call-done = bf16[16384,128]{0,1:T(8,128)(2,1)} async-done(((bf16[2048,128]{0,1:T(8,128)(2,1)}), bf16[16384,128]{0,1:T(8,128)(2,1)}) %all-gather.47.cloned.1.call-update) | async-done | bytes 4194320 | tf_op jit(solution)/shard_map/all_gather | solution.py:16
  909.9 30.2 %fusion.46 = f32[2048,128]{0,1:T(8,128)S(1)} fusion(bf16[16384,128]{0,1:T(8,128)(2,1)} %all-gather.47.cloned.1.call-done, bf16[2048,16384]{1,0:T(8,128)(2,1)} %param.5, f32[2048,128]{0,1:T(8,128)S(1)} %copy.6, f32[128]{0:T(128)S(1)} %broadcast_multiply_fusion, f32[]{:T(128)S(6)} %sub.63, f32[]{:T(128)} %bitcast), kind=kOutput, calls=%fused_computation.62 | convolution fusion | flops 8590983168 | bytes 73400840 | tf_op jit(solution)/shard_map/dot_general | solution.py:18
  (87 shorter events, 228.8 us)
Async XLA Ops:
  6.5 33.6 %all-gather.17.cloned.1.call-start = ((), (), s32[]{:S(2)}) async-start(), calls=%async_computation | async-start | bytes 4718592 | tf_op jit(solution)/shard_map/all_gather | solution.py:16
  8.7 89.0 %all-gather.19.cloned.1.call-start = ((), (), s32[]{:S(2)}) async-start(), calls=%async_computation.1 | async-start | bytes 4718592 | tf_op jit(solution)/shard_map/all_gather | solution.py:16
  28.2 42.9 %copy-start = (f32[2048,128]{1,0:T(8,128)S(1)}, f32[2048,128]{1,0:T(8,128)}, u32[]{:S(2)}) copy-start(f32[2048,128]{1,0:T(8,128)} %param.6) | copy-start | bytes 3145732
  69.7 86.4 %all-gather.21.cloned.1.call-start = ((), (), s32[]{:S(2)}) async-start(), calls=%async_computation.2 | async-start | bytes 4718592 | tf_op jit(solution)/shard_map/all_gather | solution.py:16
  128.2 85.8 %all-gather.23.cloned.1.call-start = ((), (), s32[]{:S(2)}) async-start(), calls=%async_computation.3 | async-start | bytes 4718592 | tf_op jit(solution)/shard_map/all_gather | solution.py:16
  186.2 85.8 %all-gather.25.cloned.1.call-start = ((), (), s32[]{:S(2)}) async-start(), calls=%async_computation.4 | async-start | bytes 4718592 | tf_op jit(solution)/shard_map/all_gather | solution.py:16
  244.1 85.9 %all-gather.27.cloned.1.call-start = ((), (), s32[]{:S(2)}) async-start(), calls=%async_computation.5 | async-start | bytes 4718592 | tf_op jit(solution)/shard_map/all_gather | solution.py:16
  302.1 85.9 %all-gather.29.cloned.1.call-start = ((), (), s32[]{:S(2)}) async-start(), calls=%async_computation.6 | async-start | bytes 4718592 | tf_op jit(solution)/shard_map/all_gather | solution.py:16
  360.2 85.8 %all-gather.31.cloned.1.call-start = ((), (), s32[]{:S(2)}) async-start(), calls=%async_computation.7 | async-start | bytes 4718592 | tf_op jit(solution)/shard_map/all_gather | solution.py:16
  418.1 85.9 %all-gather.33.cloned.1.call-start = ((), (), s32[]{:S(2)}) async-start(), calls=%async_computation.8 | async-start | bytes 4718592 | tf_op jit(solution)/shard_map/all_gather | solution.py:16
  476.1 85.8 %all-gather.35.cloned.1.call-start = ((), (), s32[]{:S(2)}) async-start(), calls=%async_computation.9 | async-start | bytes 4718592 | tf_op jit(solution)/shard_map/all_gather | solution.py:16
  534.1 85.8 %all-gather.37.cloned.1.call-start = ((), (), s32[]{:S(2)}) async-start(), calls=%async_computation.10 | async-start | bytes 4718592 | tf_op jit(solution)/shard_map/all_gather | solution.py:16
  592.1 85.8 %all-gather.39.cloned.1.call-start = ((), (), s32[]{:S(2)}) async-start(), calls=%async_computation.11 | async-start | bytes 4718592 | tf_op jit(solution)/shard_map/all_gather | solution.py:16
  650.1 85.9 %all-gather.41.cloned.1.call-start = ((), (), s32[]{:S(2)}) async-start(), calls=%async_computation.12 | async-start | bytes 4718592 | tf_op jit(solution)/shard_map/all_gather | solution.py:16
  708.0 85.9 %all-gather.43.cloned.1.call-start = ((), (), s32[]{:S(2)}) async-start(), calls=%async_computation.13 | async-start | bytes 4718592 | tf_op jit(solution)/shard_map/all_gather | solution.py:16
  766.1 85.9 %all-gather.45.cloned.1.call-start = ((), (), s32[]{:S(2)}) async-start(), calls=%async_computation.14 | async-start | bytes 4718592 | tf_op jit(solution)/shard_map/all_gather | solution.py:16
  824.1 85.8 %all-gather.47.cloned.1.call-start = ((), (), s32[]{:S(2)}) async-start(), calls=%async_computation.15 | async-start | bytes 4718592 | tf_op jit(solution)/shard_map/all_gather | solution.py:16
Sparse Core Ops, SparseCore 0:
  8.9 31.1 all-gather.16
  69.8 27.7 all-gather.18
  128.3 27.7 all-gather.20
  186.3 27.6 all-gather.22
  244.2 27.6 all-gather.24
  302.2 27.6 all-gather.26
  360.3 27.6 all-gather.28
  418.2 27.6 all-gather.30
  476.3 27.7 all-gather.32
  534.2 27.6 all-gather.34
  592.2 27.6 all-gather.36
  650.2 27.6 all-gather.38
  708.2 27.7 all-gather.40
  766.2 27.6 all-gather.42
  824.2 27.6 all-gather.44
  882.1 27.6 all-gather.46
where the time goes:
time: 959 us; the launch traced here: 948 us
  matrix products  502 us (52%)
  blocking collectives  204 us (21%)
  waiting for transfers between devices  201 us (21%)
  between operations  33.6 us (4%)
    dot_general x16, matrix products, local_sweeps(): prod_rows = jnp.dot(mat_rows, gathered, preferred_element_type=jnp.float32)  481 us
    psum x16, blocking collectives, local_sweeps(): lax.psum(jnp.dot(dang_float, rank_rows, preferred_element_type=jnp.float3...  204 us
    all_gather x16, waiting for transfers between devices, local_sweeps(): lax.all_gather(rank_rows.astype(jnp.bfloat16), 'row', axis=0, tiled=True)  200 us
    dot_general x16, matrix products, local_sweeps(): jnp.dot(dang_float, rank_rows, preferred_element_type=jnp.float32)  20.5 us
  transfers between devices with their start and end apart: 16, of which 16 were waited for; matrix products, arithmetic and copies ran while one was open for 2% of the time, Pallas kernels for 0%

commit v1 on v0

v1 whole, which is shorter than its diff:
```python
import functools

import jax
import jax.numpy as jnp
from jax import lax
from jax.experimental import pallas as pl
from jax.experimental.pallas import tpu as pltpu
from jax.sharding import PartitionSpec as P

MESH = pl.DeviceIdType.MESH
TILE = 256
HALVES = 2
VMEM_LIMIT = 67043328


def acc_specs(halves, tiles, rows):
    return [[pltpu.VMEM((rows, TILE), jnp.float32) for i in range(tiles)] for _ in range(halves)]


def acc_add(accs, halves, tile, count, lhs, rhs, flip):
    for i, h in enumerate(halves):
        accs[h][tile][...] += lax.dot_general(lhs[i], rhs, (((1,), (1 if flip else 0,)), ((), ())), preferred_element_type=jnp.float32)


def acc_pop(acc):
    v = acc[...]
    acc[...] = jnp.zeros_like(v)
    return v


def sweeps_kernel(n, num_sweeps, num_nodes, dang, damp, a3, e3, r3, out3, cache, gath, stream, et, rst, mcol, pm, part,
                  recv_l, recv_r, sib_own, sib_l, sib_r, send_sem, m_recv, m_send, c_sem, s_sem, io_sem):
    tiles = a3.shape[0]
    pieces, seeds, width = gath.shape[3], gath.shape[4], gath.shape[5]
    kts = width // TILE
    block = pieces * width
    pair = pieces // 2
    chunks = block // TILE
    bufs = stream.shape[0]
    lanes = et.shape[2]
    per_tile = TILE // lanes

    me = lax.axis_index("row")
    step = 1 - 2 * lax.rem(me, 2)
    sib = me + step
    right, left, opp = lax.rem(me + 2, n), lax.rem(me + n - 2, n), lax.rem(me + n // 2, n)

    def piece(slot, blk, h, p, count):
        return gath.at[slot, blk, h, pl.ds(p, count)]

    def remote(slot, blk, h, p, count, recv, dev):
        ref = piece(slot, blk, h, p, count)
        return pltpu.make_async_remote_copy(src_ref=ref, dst_ref=ref, send_sem=send_sem.at[slot], recv_sem=recv,
                                            device_id={"row": dev}, device_id_type=MESH)

    def send(*args):
        remote(*args).start()

    def arrive(slot, blk, h, p, count, recv):
        remote(slot, blk, h, p, count, recv, sib).wait_recv()

    def wait_sends(slot):
        ref = gath.at[slot, pl.ds(0, n - 1)]
        pltpu.make_async_copy(ref, ref, send_sem.at[slot]).wait()

    def others(fn):
        for k in range(1, n):
            fn(lax.rem(me + k, n))

    def stream_copy(c):
        blk = me + (c // chunks) * (sib - me)
        col = pl.multiple_of(blk * block + lax.rem(c, chunks) * TILE, TILE)
        b = lax.rem(c, bufs)
        return pltpu.make_async_copy(a3.at[:, :, pl.ds(col, TILE)], stream.at[b], s_sem.at[b])

    def cache_copy(ci, kt, blk, p):
        col = pl.multiple_of(blk * block + p * width + kt * TILE, TILE)
        return pltpu.make_async_copy(a3.at[:, :, pl.ds(col, TILE)], cache.at[ci, kt], c_sem.at[ci, kt])

    blocks = [left, right, left + step, right + step, opp, opp + step]

    def entry(accs):
        barrier = pltpu.get_barrier_semaphore()
        others(lambda dev: pl.semaphore_signal(barrier, inc=1, device_id={"row": dev}, device_id_type=MESH))
        load_r = pltpu.make_async_copy(r3, rst, io_sem.at[0])
        load_e = pltpu.make_async_copy(e3, et, io_sem.at[1])
        load_r.start()
        load_e.start()
        for c in range(bufs):
            stream_copy(c).start()

        def start_cache(b, p):
            for kt in range(kts):
                cache_copy(b * pieces + p, kt, blocks[b], p).start()

        for i in range(2):
            for b in range(4):
                for j in range(pair):
                    start_cache(b, (i if b % 2 == 0 else 1 - i) * pair + j)
        for b in (4, 5):
            for j in range(pair):
                start_cache(b, j)
                start_cache(b, pair + j)
        for h in range(HALVES):
            for i in range(tiles):
                acc_pop(accs[h][i])

        def send_own(slot, h, u):
            if u == 0:
                send(slot, me, h, 0, pair, recv_l.at[slot, 2 * h], right)
                send(slot, me, h, 0, pair, sib_own.at[slot, 2 * h], sib)
            else:
                send(slot, me, h, pair, pair, recv_r.at[slot, 2 * h], left)
                send(slot, me, h, pair, pair, recv_l.at[slot, 2 * h + 1], right)
                send(slot, me, h, 0, pair, recv_r.at[slot, 2 * h + 1], left)
                send(slot, me, h, pair, pair, sib_own.at[slot, 2 * h + 1], sib)

        def pm_copy(slot, dev):
            return pltpu.make_async_remote_copy(src_ref=pm.at[slot, me], dst_ref=pm.at[slot, me], send_sem=m_send.at[slot],
                                                recv_sem=m_recv.at[slot], device_id={"row": dev}, device_id_type=MESH)

        def send_mass(slot):
            mass = jnp.sum(part[...], axis=1, keepdims=True)
            pm[slot, me] = jnp.transpose(jnp.broadcast_to(mass, (HALVES * seeds, lanes)))[: pm.shape[2]]
            others(lambda dev: pm_copy(slot, dev).start())

        def wait_mass(slot):
            ref = pm.at[slot, pl.ds(0, n - 1)]
            pltpu.make_async_copy(ref, ref, m_recv.at[slot]).wait()
            pltpu.make_async_copy(ref, ref, m_send.at[slot]).wait()

        def put(slot, h, j, val):
            p, off = j * lanes // width, j * lanes % width
            gath[slot, me, h, p, :, off : off + lanes] = val.astype(jnp.bfloat16)
            rst[j, h * seeds : (h + 1) * seeds, :] = val
            return val * dang[j : j + 1, :].astype(jnp.float32)

        node_tiles = block // lanes

        load_r.wait()
        pl.semaphore_wait(barrier, n - 1)
        for j in range(node_tiles):
            rst[j] = jnp.transpose(rst[j])
        for h in range(HALVES):
            total = jnp.zeros((seeds, lanes), jnp.float32)
            for j in range(node_tiles):
                total += put(0, h, j, rst[j, h * seeds : (h + 1) * seeds, :])
                if j == node_tiles // 2 - 1:
                    send_own(0, h, 0)
            send_own(0, h, 1)
            part[h * seeds : (h + 1) * seeds, :] = total
        send_mass(0)
        load_e.wait()
        for j in range(node_tiles):
            et[j] = jnp.transpose(et[j])

        def compute(first, slot, items, halves):
            count = 0
            for b, p in items:
                lhs = [gath[slot, blocks[b], h, p] for h in halves]
                for kt in range(kts):
                    if first:
                        cache_copy(b * pieces + p, kt, blocks[b], p).wait()
                    cut = [v[:, kt * TILE : (kt + 1) * TILE] for v in lhs]
                    for i in range(tiles):
                        rhs = cache[b * pieces + p, kt, i]
                        if first:
                            rhs = jnp.transpose(rhs)
                            cache[b * pieces + p, kt, i] = rhs
                        acc_add(accs, halves, i, count + i // 2, cut, rhs, False)
                    count += tiles // 2

        def near(slot, blk, base):
            def trip(i, carry):
                count = 0
                for j in range(bufs):
                    c = base + i * bufs + j
                    p = i * (bufs // kts) + j // kts
                    stream_copy(c).wait()
                    cut = [gath[slot, blk, h, p, :, (j % kts) * TILE : (j % kts + 1) * TILE] for h in range(HALVES)]
                    for k in range(tiles):
                        acc_add(accs, range(HALVES), k, count + k // 2, cut, stream[j, k], True)
                    count += tiles // 2
                    stream_copy(lax.rem(c + bufs, 2 * chunks)).start()
                return carry

            lax.fori_loop(0, chunks // bufs, trip, 0)

        def finish(t, slot, h):
            nxt = 1 - slot
            factor = damp[t]
            rows = slice(h * seeds, (h + 1) * seeds)
            total = jnp.zeros((seeds, lanes), jnp.float32)
            mass = mcol[rows, :] * (factor / num_nodes)
            for i in range(tiles):
                prod = acc_pop(accs[h][i])
                for k in range(per_tile):
                    j = i * per_tile + k
                    val = factor * prod[:, k * lanes : (k + 1) * lanes] + (1.0 - factor) * et[j, rows, :] + mass
                    total += put(nxt, h, j, val)
                if i == tiles // 2 - 1:
                    pl.when(t < num_sweeps - 1)(lambda: send_own(nxt, h, 0))
            pl.when(t < num_sweeps - 1)(lambda: send_own(nxt, h, 1))
            part[rows, :] = total

        def sweep(t, slot, first):
            near(slot, me, 0)
            for h in range(HALVES):
                for u in range(2):
                    arrive(slot, sib, h, u * pair, pair, sib_own.at[slot, 2 * h + u])
            near(slot, sib, chunks)
            if not first:
                wait_sends(1 - slot)

            def pass_on(h, i):
                arrive(slot, left, h, i * pair, pair, recv_l.at[slot, 2 * h + i])
                if i == 0:
                    for j in range(pair):
                        send(slot, left, h, j, 1, recv_l.at[slot, 4 + 2 * h + j], right)
                arrive(slot, right, h, (1 - i) * pair, pair, recv_r.at[slot, 2 * h + i])
                if i == 0:
                    for j in range(pair):
                        send(slot, right, h, pair + j, 1, recv_r.at[slot, 4 + 2 * h + j], left)
                send(slot, left, h, i * pair, pair, sib_l.at[slot, 2 * h + i], sib)
                send(slot, right, h, (1 - i) * pair, pair, sib_r.at[slot, 2 * h + i], sib)

            pass_on(0, 0)
            pass_on(0, 1)
            for i in range(2):
                pass_on(1, i)

                def direct(j, carry):
                    compute(first, slot, [(0, i * pair + j), (1, (1 - i) * pair + j)], range(HALVES))
                    return carry

                lax.fori_loop(0, pair, direct, 0)
                for h in range(HALVES):
                    arrive(slot, blocks[2], h, i * pair, pair, sib_l.at[slot, 2 * h + i])
                    arrive(slot, blocks[3], h, (1 - i) * pair, pair, sib_r.at[slot, 2 * h + i])

                def through(j, carry):
                    compute(first, slot, [(2, i * pair + j), (3, (1 - i) * pair + j)], range(HALVES))
                    return carry

                lax.fori_loop(0, pair, through, 0)

            wait_mass(slot)
            row = jnp.sum(pm[slot], axis=0)[0:1]
            mcol[...] = jnp.transpose(jnp.broadcast_to(row, (lanes, HALVES * seeds)))
            for h in range(HALVES):

                def direct(j, carry):
                    k = 4 + 2 * h + j
                    arrive(slot, opp, h, j, 1, recv_l.at[slot, k])
                    send(slot, opp, h, j, 1, sib_l.at[slot, k], sib)
                    arrive(slot, opp, h, pair + j, 1, recv_r.at[slot, k])
                    send(slot, opp, h, pair + j, 1, sib_r.at[slot, k], sib)
                    compute(first and h == 0, slot, [(4, j), (4, pair + j)], [h])
                    return carry

                lax.fori_loop(0, pair, direct, 0)

                def through(j, carry):
                    k = 4 + 2 * h + j
                    arrive(slot, blocks[5], h, j, 1, sib_l.at[slot, k])
                    arrive(slot, blocks[5], h, pair + j, 1, sib_r.at[slot, k])
                    compute(first and h == 0, slot, [(5, j), (5, pair + j)], [h])
                    return carry

                lax.fori_loop(0, pair, through, 0)
                finish(t, slot, h)
            pl.when(t < num_sweeps - 1)(lambda: send_mass(1 - slot))

        sweep(0, 0, True)

        def trip(t, carry):
            sweep(t, lax.rem(t, 2), False)
            return carry

        lax.fori_loop(1, num_sweeps, trip, 0)

        wait_sends((num_sweeps - 1) % 2)
        for c in range(bufs):
            stream_copy(c).wait()
        for j in range(node_tiles):
            rst[j] = jnp.transpose(rst[j])
        store = pltpu.make_async_copy(rst, out3, io_sem.at[0])
        store.start()
        store.wait()

    pl.run_scoped(entry, acc_specs(HALVES, tiles, seeds))


def solution(mesh):
    n = mesh.shape["row"]
    spec_rows = P(("batch", "row"), None)
    spec_vec = P(("batch", "row"))

    def local_sweeps(mat_rows, tele_rows, dang_rows, damping, start_rows):
        rows, num_nodes = mat_rows.shape
        num_seeds = start_rows.shape[1]
        lanes, width, bufs = 128, 512, 4
        assert n == 8 and rows * n == num_nodes and num_seeds == lanes
        tiles, pieces = rows // TILE, rows // width
        f32, bf16 = jnp.float32, jnp.bfloat16
        tile3 = (rows // lanes, lanes, num_seeds)
        dma, hbm = pltpu.SemaphoreType.DMA, pl.BlockSpec(memory_space=pl.ANY)
        out = pl.pallas_call(
            functools.partial(sweeps_kernel, n, damping.shape[0], num_nodes),
            out_shape=jax.ShapeDtypeStruct(tile3, f32),
            in_specs=[pl.BlockSpec(memory_space=pltpu.VMEM), pl.BlockSpec(memory_space=pltpu.SMEM), hbm, hbm, hbm],
            out_specs=hbm,
            scratch_shapes=[
                pltpu.VMEM(((n - 2) * pieces, width // TILE, tiles, TILE, TILE), bf16),
                pltpu.VMEM((2, n, HALVES, pieces, num_seeds // HALVES, width), bf16),
                pltpu.VMEM((bufs, tiles, TILE, TILE), bf16),
                pltpu.VMEM(tile3, f32),
                pltpu.VMEM(tile3, f32),
                pltpu.VMEM((num_seeds, lanes), f32),
                pltpu.VMEM((2, n, 8, lanes), f32),
                pltpu.VMEM((num_seeds, lanes), f32),
                dma((2, 8)), dma((2, 8)), dma((2, 4)), dma((2, 8)), dma((2, 8)),
                dma((2,)), dma((2,)), dma((2,)),
                dma(((n - 2) * pieces, width // TILE)), dma((bufs,)), dma((2,)),
            ],
            compiler_params=pltpu.CompilerParams(collective_id=0, has_side_effects=True, vmem_limit_bytes=VMEM_LIMIT),
        )(
            dang_rows.reshape(rows // lanes, lanes),
            damping,
            mat_rows.reshape(tiles, TILE, num_nodes),
            tele_rows.reshape(tile3),
            start_rows.reshape(tile3),
        )
        return out.reshape(rows, num_seeds)

    return jax.shard_map(local_sweeps, mesh=mesh, in_specs=(spec_rows, spec_rows, spec_vec, P(None), spec_rows), out_specs=spec_rows, check_vma=False)
```

time: 959 us -> 530 us (0.55); the launches traced: 948 us -> 530 us
  Pallas kernels: 0 us -> 528 us
  matrix products: 502 us -> 0 us
  blocking collectives: 204 us -> 0 us
  waiting for transfers between devices: 201 us -> 0 us
  between operations: 33.6 us -> 0.01 us
    pallas_call x0 -> x1, Pallas kernels: none -> 528 us  [local_sweeps(): pl.pallas_call(functools.partial(sweeps_kernel, n, damping.shape[0], num_...]
    dot_general x32 -> x0, matrix products: 502 us -> none  [the longest x16 481 us: local_sweeps(): prod_rows = jnp.dot(mat_rows, gathered, preferred_element_type=jnp.float32)]
    psum x16 -> x0, blocking collectives: 204 us -> none  [local_sweeps(): lax.psum(jnp.dot(dang_float, rank_rows, preferred_element_type=jnp.float3...]
    all_gather x16 -> x0, waiting for transfers between devices: 200 us -> none  [local_sweeps(): lax.all_gather(rank_rows.astype(jnp.bfloat16), 'row', axis=0, tiled=True)]
  transfers between devices with their start and end apart: 16 -> 0, of which waited for: 16 -> 0; matrix products, arithmetic and copies ran while one was open for 2% -> 0% of each run, Pallas kernels for 0% -> 0%
where the time goes in v1:
time: 530 us
  Pallas kernels  528 us (100%)
    pallas_call x1, Pallas kernels, local_sweeps(): pl.pallas_call(functools.partial(sweeps_kernel, n, damping.shape[0], num_...  528 us

profile of v1, /device:TPU:113, one launch (start us, length us, event | category | flops | bytes accessed | tf_op | source)
XLA Modules:
  0.0 530.3 jit_solution(11164375978629502417)
XLA Ops:
  0.0 528.0 %shard_map.55 = f32[16,128,128]{2,1,0:T(8,128)} custom-call(s32[16,128]{1,0:T(8,128)} %bitcast.8, f32[16]{0:T(128)} %damp.1, bf16[8,256,16384]{2,1,0:T(8,128)(2,1)} %bitcast.1.a3, f32[16,128,128]{2,1,0:T(8,128)} %bitcast.6, f32[16,128,128]{2,1,0:T(8,128)} %bitcast.7), custom_call_target="tpu_custom_call" | custom-call | tf_op jit(solution)/shard_map/pallas_call | solution.py:308
  528.1 2.3 copy.7

commit v2 on v1

--- a/solution.py
+++ b/solution.py
@@ -13,22 +13,11 @@
 VMEM_LIMIT = 67043328
 
 
-def acc_specs(halves, tiles, rows):
-    return [[pltpu.VMEM((rows, TILE), jnp.float32) for i in range(tiles)] for _ in range(halves)]
-
-
-def acc_add(accs, halves, tile, count, lhs, rhs, flip):
-    for i, h in enumerate(halves):
-        accs[h][tile][...] += lax.dot_general(lhs[i], rhs, (((1,), (1 if flip else 0,)), ((), ())), preferred_element_type=jnp.float32)
-
-
-def acc_pop(acc):
-    v = acc[...]
-    acc[...] = jnp.zeros_like(v)
-    return v
-
-
-def sweeps_kernel(n, num_sweeps, num_nodes, dang, damp, a3, e3, r3, out3, cache, gath, stream, et, rst, mcol, pm, part,
+def product(lhs, rhs, flip):
+    return lax.dot_general(lhs, rhs, (((1,), (1 if flip else 0,)), ((), ())), preferred_element_type=jnp.float32)
+
+
+def sweeps_kernel(n, num_sweeps, num_nodes, dang, damp, a3, e3, r3, out3, cache, gath, stream, et, acc, mcol, pm, part,
                   recv_l, recv_r, sib_own, sib_l, sib_r, send_sem, m_recv, m_send, c_sem, s_sem, io_sem):
     tiles = a3.shape[0]
     pieces, seeds, width = gath.shape[3], gath.shape[4], gath.shape[5]
@@ -79,31 +68,29 @@
 
     blocks = [left, right, left + step, right + step, opp, opp + step]
 
-    def entry(accs):
+    def entry():
         barrier = pltpu.get_barrier_semaphore()
         others(lambda dev: pl.semaphore_signal(barrier, inc=1, device_id={"row": dev}, device_id_type=MESH))
-        load_r = pltpu.make_async_copy(r3, rst, io_sem.at[0])
+        load_r = pltpu.make_async_copy(r3, acc, io_sem.at[0])
         load_e = pltpu.make_async_copy(e3, et, io_sem.at[1])
         load_r.start()
         load_e.start()
         for c in range(bufs):
             stream_copy(c).start()
 
-        def start_cache(b, p):
-            for kt in range(kts):
-                cache_copy(b * pieces + p, kt, blocks[b], p).start()
-
-        for i in range(2):
-            for b in range(4):
+        def load_cache():
+            def start_cache(b, p):
+                for kt in range(kts):
+                    cache_copy(b * pieces + p, kt, blocks[b], p).start()
+
+            for i in range(2):
+                for b in range(4):
+                    for j in range(pair):
+                        start_cache(b, (i if b % 2 == 0 else 1 - i) * pair + j)
+            for b in (4, 5):
                 for j in range(pair):
-                    start_cache(b, (i if b % 2 == 0 else 1 - i) * pair + j)
-        for b in (4, 5):
-            for j in range(pair):
-                start_cache(b, j)
-                start_cache(b, pair + j)
-        for h in range(HALVES):
-            for i in range(tiles):
-                acc_pop(accs[h][i])
+                    start_cache(b, j)
+                    start_cache(b, pair + j)
 
         def send_own(slot, h, u):
             if u == 0:
@@ -132,7 +119,7 @@
         def put(slot, h, j, val):
             p, off = j * lanes // width, j * lanes % width
             gath[slot, me, h, p, :, off : off + lanes] = val.astype(jnp.bfloat16)
-            rst[j, h * seeds : (h + 1) * seeds, :] = val
+            acc[j, h * seeds : (h + 1) * seeds, :] = val
             return val * dang[j : j + 1, :].astype(jnp.float32)
 
         node_tiles = block // lanes
@@ -140,11 +127,11 @@
         load_r.wait()
         pl.semaphore_wait(barrier, n - 1)
         for j in range(node_tiles):
-            rst[j] = jnp.transpose(rst[j])
+            acc[j] = jnp.transpose(acc[j])
         for h in range(HALVES):
             total = jnp.zeros((seeds, lanes), jnp.float32)
             for j in range(node_tiles):
-                total += put(0, h, j, rst[j, h * seeds : (h + 1) * seeds, :])
+                total += put(0, h, j, acc[j, h * seeds : (h + 1) * seeds, :])
                 if j == node_tiles // 2 - 1:
                     send_own(0, h, 0)
             send_own(0, h, 1)
@@ -154,37 +141,55 @@
         for j in range(node_tiles):
             et[j] = jnp.transpose(et[j])
 
+        def add(i, rows, val, fresh):
+            for k in range(per_tile):
+                j = i * per_tile + k
+                cut = val[:, k * lanes : (k + 1) * lanes]
+                acc[j, rows, :] = cut if fresh else acc[j, rows, :] + cut
+
+        def left_side(slot, blk, halves, p, kt):
+            cuts = [gath[slot, blk, h, p, :, kt * TILE : (kt + 1) * TILE] for h in halves]
+            return cuts[0] if len(cuts) == 1 else jnp.concatenate(cuts, axis=0)
+
         def compute(first, slot, items, halves):
-            count = 0
-            for b, p in items:
-                lhs = [gath[slot, blocks[b], h, p] for h in halves]
-                for kt in range(kts):
-                    if first:
+            rows = slice(halves[0] * seeds, (halves[-1] + 1) * seeds)
+            if first:
+                for b, p in items:
+                    for kt in range(kts):
                         cache_copy(b * pieces + p, kt, blocks[b], p).wait()
-                    cut = [v[:, kt * TILE : (kt + 1) * TILE] for v in lhs]
-                    for i in range(tiles):
+            for i in range(tiles):
+                val = None
+                for b, p in items:
+                    for kt in range(kts):
                         rhs = cache[b * pieces + p, kt, i]
                         if first:
                             rhs = jnp.transpose(rhs)
                             cache[b * pieces + p, kt, i] = rhs
-                        acc_add(accs, halves, i, count + i // 2, cut, rhs, False)
-                    count += tiles // 2
+                        term = product(left_side(slot, blocks[b], halves, p, kt), rhs, False)
+                        val = term if val is None else val + term
+                add(i, rows, val, False)
 
         def near(slot, blk, base):
+            rows = slice(0, HALVES * seeds)
+
+            def chunk(i, j, fresh):
+                c = base + i * bufs + j
+                p = i * (bufs // kts) + j // kts
+                stream_copy(c).wait()
+                lhs = left_side(slot, blk, range(HALVES), p, j % kts)
+                for k in range(tiles):
+                    add(k, rows, product(lhs, stream[j, k], True), fresh)
+                stream_copy(lax.rem(c + bufs, 2 * chunks)).start()
+
             def trip(i, carry):
-                count = 0
                 for j in range(bufs):
-                    c = base + i * bufs + j
-                    p = i * (bufs // kts) + j // kts
-                    stream_copy(c).wait()
-                    cut = [gath[slot, blk, h, p, :, (j % kts) * TILE : (j % kts + 1) * TILE] for h in range(HALVES)]
-                    for k in range(tiles):
-                        acc_add(accs, range(HALVES), k, count + k // 2, cut, stream[j, k], True)
-                    count += tiles // 2
-                    stream_copy(lax.rem(c + bufs, 2 * chunks)).start()
+                    chunk(i, j, False)
                 return carry
 
-            lax.fori_loop(0, chunks // bufs, trip, 0)
+            if base == 0:
+                for j in range(bufs):
+                    chunk(0, j, j == 0)
+            lax.fori_loop(1 if base == 0 else 0, chunks // bufs, trip, 0)
 
         def finish(t, slot, h):
             nxt = 1 - slot
@@ -193,10 +198,9 @@
             total = jnp.zeros((seeds, lanes), jnp.float32)
             mass = mcol[rows, :] * (factor / num_nodes)
             for i in range(tiles):
-                prod = acc_pop(accs[h][i])
                 for k in range(per_tile):
                     j = i * per_tile + k
-                    val = factor * prod[:, k * lanes : (k + 1) * lanes] + (1.0 - factor) * et[j, rows, :] + mass
+                    val = factor * acc[j, rows, :] + (1.0 - factor) * et[j, rows, :] + mass
                     total += put(nxt, h, j, val)
                 if i == tiles // 2 - 1:
                     pl.when(t < num_sweeps - 1)(lambda: send_own(nxt, h, 0))
@@ -209,7 +213,9 @@
                 for u in range(2):
                     arrive(slot, sib, h, u * pair, pair, sib_own.at[slot, 2 * h + u])
             near(slot, sib, chunks)
-            if not first:
+            if first:
+                load_cache()
+            else:
                 wait_sends(1 - slot)
 
             def pass_on(h, i):
@@ -228,21 +234,11 @@
             pass_on(0, 1)
             for i in range(2):
                 pass_on(1, i)
-
-                def direct(j, carry):
-                    compute(first, slot, [(0, i * pair + j), (1, (1 - i) * pair + j)], range(HALVES))
-                    return carry
-
-                lax.fori_loop(0, pair, direct, 0)
+                compute(first, slot, [(b, (i if b == 0 else 1 - i) * pair + j) for b in (0, 1) for j in range(pair)], range(HALVES))
                 for h in range(HALVES):
                     arrive(slot, blocks[2], h, i * pair, pair, sib_l.at[slot, 2 * h + i])
                     arrive(slot, blocks[3], h, (1 - i) * pair, pair, sib_r.at[slot, 2 * h + i])
-
-                def through(j, carry):
-                    compute(first, slot, [(2, i * pair + j), (3, (1 - i) * pair + j)], range(HALVES))
-                    return carry
-
-                lax.fori_loop(0, pair, through, 0)
+                compute(first, slot, [(b, (i if b == 2 else 1 - i) * pair + j) for b in (2, 3) for j in range(pair)], range(HALVES))
 
             wait_mass(slot)
             row = jnp.sum(pm[slot], axis=0)[0:1]
@@ -283,12 +279,12 @@
         for c in range(bufs):
             stream_copy(c).wait()
         for j in range(node_tiles):
-            rst[j] = jnp.transpose(rst[j])
-        store = pltpu.make_async_copy(rst, out3, io_sem.at[0])
+            acc[j] = jnp.transpose(acc[j])
+        store = pltpu.make_async_copy(acc, out3, io_sem.at[0])
         store.start()
         store.wait()
 
-    pl.run_scoped(entry, acc_specs(HALVES, tiles, seeds))
+    entry()
 
 
 def solution(mesh):

time: 530 us -> 351 us (0.66)
  Pallas kernels: 528 us -> 349 us
    pallas_call x1, Pallas kernels: 528 us -> 349 us  [local_sweeps(): pl.pallas_call(functools.partial(sweeps_kernel, n, damping.shape[0], num_...]
where the time goes in v2:
time: 351 us
  Pallas kernels  349 us (99%)
    pallas_call x1, Pallas kernels, local_sweeps(): pl.pallas_call(functools.partial(sweeps_kernel, n, damping.shape[0], num_...  349 us

profile of v2, /device:TPU:113, one launch (start us, length us, event | category | flops | bytes accessed | tf_op | source)
XLA Modules:
  0.0 351.1 jit_solution(12508929731233726751)
XLA Ops:
  0.0 348.8 %shard_map.55 = f32[16,128,128]{2,1,0:T(8,128)} custom-call(s32[16,128]{1,0:T(8,128)} %bitcast.8, f32[16]{0:T(128)} %damp.1, bf16[8,256,16384]{2,1,0:T(8,128)(2,1)} %bitcast.1.a3, f32[16,128,128]{2,1,0:T(8,128)} %bitcast.6, f32[16,128,128]{2,1,0:T(8,128)} %bitcast.7), custom_call_target="tpu_custom_call" | custom-call | tf_op jit(solution)/shard_map/pallas_call | solution.py:304
  348.8 2.3 copy.7

commit v3 on v2

--- a/solution.py
+++ b/solution.py
@@ -83,7 +83,7 @@
                 for kt in range(kts):
                     cache_copy(b * pieces + p, kt, blocks[b], p).start()
 
-            for i in range(2):
+            for i in (1, 0):
                 for b in range(4):
                     for j in range(pair):
                         start_cache(b, (i if b % 2 == 0 else 1 - i) * pair + j)
@@ -98,9 +98,13 @@
                 send(slot, me, h, 0, pair, sib_own.at[slot, 2 * h], sib)
             else:
                 send(slot, me, h, pair, pair, recv_r.at[slot, 2 * h], left)
-                send(slot, me, h, pair, pair, recv_l.at[slot, 2 * h + 1], right)
-                send(slot, me, h, 0, pair, recv_r.at[slot, 2 * h + 1], left)
+                if h == 0:
+                    send_second(slot, h)
                 send(slot, me, h, pair, pair, sib_own.at[slot, 2 * h + 1], sib)
+
+        def send_second(slot, h):
+            send(slot, me, h, pair, pair, recv_l.at[slot, 2 * h + 1], right)
+            send(slot, me, h, 0, pair, recv_r.at[slot, 2 * h + 1], left)
 
         def pm_copy(slot, dev):
             return pltpu.make_async_remote_copy(src_ref=pm.at[slot, me], dst_ref=pm.at[slot, me], send_sem=m_send.at[slot],
@@ -169,27 +173,16 @@
                         val = term if val is None else val + term
                 add(i, rows, val, False)
 
-        def near(slot, blk, base):
+        def near(slot, blk, group):
             rows = slice(0, HALVES * seeds)
-
-            def chunk(i, j, fresh):
-                c = base + i * bufs + j
-                p = i * (bufs // kts) + j // kts
+            base = group * bufs
+            for j in range(bufs):
+                c = base + j
                 stream_copy(c).wait()
-                lhs = left_side(slot, blk, range(HALVES), p, j % kts)
+                lhs = left_side(slot, blk, range(HALVES), c % chunks // kts, j % kts)
                 for k in range(tiles):
-                    add(k, rows, product(lhs, stream[j, k], True), fresh)
-                stream_copy(lax.rem(c + bufs, 2 * chunks)).start()
-
-            def trip(i, carry):
-                for j in range(bufs):
-                    chunk(i, j, False)
-                return carry
-
-            if base == 0:
-                for j in range(bufs):
-                    chunk(0, j, j == 0)
-            lax.fori_loop(1 if base == 0 else 0, chunks // bufs, trip, 0)
+                    add(k, rows, product(lhs, stream[j, k], True), c == 0)
+                stream_copy((c + bufs) % (2 * chunks)).start()
 
         def finish(t, slot, h):
             nxt = 1 - slot
@@ -208,15 +201,7 @@
             part[rows, :] = total
 
         def sweep(t, slot, first):
-            near(slot, me, 0)
-            for h in range(HALVES):
-                for u in range(2):
-                    arrive(slot, sib, h, u * pair, pair, sib_own.at[slot, 2 * h + u])
-            near(slot, sib, chunks)
-            if first:
-                load_cache()
-            else:
-                wait_sends(1 - slot)
+            both = range(HALVES)
 
             def pass_on(h, i):
                 arrive(slot, left, h, i * pair, pair, recv_l.at[slot, 2 * h + i])
@@ -227,44 +212,78 @@
                 if i == 0:
                     for j in range(pair):
                         send(slot, right, h, pair + j, 1, recv_r.at[slot, 4 + 2 * h + j], left)
+                    if h == 0:
+                        send_second(slot, 1)
                 send(slot, left, h, i * pair, pair, sib_l.at[slot, 2 * h + i], sib)
                 send(slot, right, h, (1 - i) * pair, pair, sib_r.at[slot, 2 * h + i], sib)
 
+            def pass_far(h, j):
+                k = 4 + 2 * h + j
+                arrive(slot, opp, h, j, 1, recv_l.at[slot, k])
+                send(slot, opp, h, j, 1, sib_l.at[slot, k], sib)
+                arrive(slot, opp, h, pair + j, 1, recv_r.at[slot, k])
+                send(slot, opp, h, pair + j, 1, sib_r.at[slot, k], sib)
+
+            def around(b, i, halves, turn):
+                if b == 2:
+                    for h in halves:
+                        arrive(slot, blocks[2], h, i * pair, pair, sib_l.at[slot, 2 * h + i])
+                        arrive(slot, blocks[3], h, (1 - i) * pair, pair, sib_r.at[slot, 2 * h + i])
+                items = [(b + k, (i if k == 0 else 1 - i) * pair + j) for k in range(2) for j in range(pair)]
+                compute(turn, slot, items, halves)
+
+            def far(b, h, turn):
+                if first:
+
+                    def trip(j, carry):
+                        if b == 5:
+                            arrive(slot, blocks[5], h, j, 1, sib_l.at[slot, 4 + 2 * h + j])
+                            arrive(slot, blocks[5], h, pair + j, 1, sib_r.at[slot, 4 + 2 * h + j])
+                        compute(turn, slot, [(b, j), (b, pair + j)], [h])
+                        return carry
+
+                    lax.fori_loop(0, pair, trip, 0)
+                else:
+                    if b == 5:
+                        for j in range(pair):
+                            arrive(slot, blocks[5], h, j, 1, sib_l.at[slot, 4 + 2 * h + j])
+                            arrive(slot, blocks[5], h, pair + j, 1, sib_r.at[slot, 4 + 2 * h + j])
+                    compute(turn, slot, [(b, p) for p in range(pieces)], [h])
+
+            near(slot, me, 0)
+            if not first:
+                wait_sends(1 - slot)
             pass_on(0, 0)
+            near(slot, me, 1)
+            for h in both:
+                for u in range(2):
+                    arrive(slot, sib, h, u * pair, pair, sib_own.at[slot, 2 * h + u])
+            near(slot, sib, 2)
             pass_on(0, 1)
-            for i in range(2):
-                pass_on(1, i)
-                compute(first, slot, [(b, (i if b == 0 else 1 - i) * pair + j) for b in (0, 1) for j in range(pair)], range(HALVES))
-                for h in range(HALVES):
-                    arrive(slot, blocks[2], h, i * pair, pair, sib_l.at[slot, 2 * h + i])
-                    arrive(slot, blocks[3], h, (1 - i) * pair, pair, sib_r.at[slot, 2 * h + i])
-                compute(first, slot, [(b, (i if b == 2 else 1 - i) * pair + j) for b in (2, 3) for j in range(pair)], range(HALVES))
-
+            near(slot, sib, 3)
+            if first:
+                load_cache()
+            around(0, 1, [0], first)
+            pass_on(1, 0)
+            around(2, 1, [0], first)
+            pass_far(0, 0)
+            around(0, 0, both, first)
+            pass_far(0, 1)
+            around(2, 0, both, first)
             wait_mass(slot)
             row = jnp.sum(pm[slot], axis=0)[0:1]
             mcol[...] = jnp.transpose(jnp.broadcast_to(row, (lanes, HALVES * seeds)))
-            for h in range(HALVES):
-
-                def direct(j, carry):
-                    k = 4 + 2 * h + j
-                    arrive(slot, opp, h, j, 1, recv_l.at[slot, k])
-                    send(slot, opp, h, j, 1, sib_l.at[slot, k], sib)
-                    arrive(slot, opp, h, pair + j, 1, recv_r.at[slot, k])
-                    send(slot, opp, h, pair + j, 1, sib_r.at[slot, k], sib)
-                    compute(first and h == 0, slot, [(4, j), (4, pair + j)], [h])
-                    return carry
-
-                lax.fori_loop(0, pair, direct, 0)
-
-                def through(j, carry):
-                    k = 4 + 2 * h + j
-                    arrive(slot, blocks[5], h, j, 1, sib_l.at[slot, k])
-                    arrive(slot, blocks[5], h, pair + j, 1, sib_r.at[slot, k])
-                    compute(first and h == 0, slot, [(5, j), (5, pair + j)], [h])
-                    return carry
-
-                lax.fori_loop(0, pair, through, 0)
-                finish(t, slot, h)
+            far(4, 0, first)
+            far(5, 0, first)
+            finish(t, slot, 0)
+            pass_on(1, 1)
+            around(0, 1, [1], False)
+            pass_far(1, 0)
+            around(2, 1, [1], False)
+            pass_far(1, 1)
+            far(4, 1, False)
+            far(5, 1, False)
+            finish(t, slot, 1)
             pl.when(t < num_sweeps - 1)(lambda: send_mass(1 - slot))
 
         sweep(0, 0, True)

time: 351 us -> 366 us (1.043)
  Pallas kernels: 349 us -> 364 us
    pallas_call x1, Pallas kernels: 349 us -> 364 us  [local_sweeps(): pl.pallas_call(functools.partial(sweeps_kernel, n, damping.shape[0], num_...]
where the time goes in v3:
time: 366 us
  Pallas kernels  364 us (99%)
    pallas_call x1, Pallas kernels, local_sweeps(): pl.pallas_call(functools.partial(sweeps_kernel, n, damping.shape[0], num_...  364 us

profile of v3, /device:TPU:113, one launch (start us, length us, event | category | flops | bytes accessed | tf_op | source)
XLA Modules:
  0.0 366.1 jit_solution(2043706040478431159)
XLA Ops:
  0.0 363.8 %shard_map.55 = f32[16,128,128]{2,1,0:T(8,128)} custom-call(s32[16,128]{1,0:T(8,128)} %bitcast.8, f32[16]{0:T(128)} %damp.1, bf16[8,256,16384]{2,1,0:T(8,128)(2,1)} %bitcast.1.a3, f32[16,128,128]{2,1,0:T(8,128)} %bitcast.6, f32[16,128,128]{2,1,0:T(8,128)} %bitcast.7), custom_call_target="tpu_custom_call" | custom-call | tf_op jit(solution)/shard_map/pallas_call | solution.py:323
  363.8 2.3 copy.7

commit v4 on v3

--- a/solution.py
+++ b/solution.py
@@ -17,8 +17,8 @@
     return lax.dot_general(lhs, rhs, (((1,), (1 if flip else 0,)), ((), ())), preferred_element_type=jnp.float32)
 
 
-def sweeps_kernel(n, num_sweeps, num_nodes, dang, damp, a3, e3, r3, out3, cache, gath, stream, et, acc, mcol, pm, part,
-                  recv_l, recv_r, sib_own, sib_l, sib_r, send_sem, m_recv, m_send, c_sem, s_sem, io_sem):
+def sweeps_kernel(n, num_sweeps, num_nodes, dang, damp, a3, e3, r3, out3, turned, cache, gath, stream, et, acc, mcol, pm, part,
+                  recv_l, recv_r, sib_own, sib_l, sib_r, send_sem, m_recv, m_send, c_sem, s_sem, t_sem, io_sem):
     tiles = a3.shape[0]
     pieces, seeds, width = gath.shape[3], gath.shape[4], gath.shape[5]
     kts = width // TILE
@@ -61,6 +61,14 @@
         col = pl.multiple_of(blk * block + lax.rem(c, chunks) * TILE, TILE)
         b = lax.rem(c, bufs)
         return pltpu.make_async_copy(a3.at[:, :, pl.ds(col, TILE)], stream.at[b], s_sem.at[b])
+
+    def turned_copy(c):
+        b = lax.rem(c, bufs)
+        return pltpu.make_async_copy(turned.at[c], stream.at[b], s_sem.at[b])
+
+    def turned_store(c):
+        b = lax.rem(c, bufs)
+        return pltpu.make_async_copy(stream.at[b], turned.at[c], t_sem.at[b])
 
     def cache_copy(ci, kt, blk, p):
         col = pl.multiple_of(blk * block + p * width + kt * TILE, TILE)
@@ -141,6 +149,7 @@
             send_own(0, h, 1)
             part[h * seeds : (h + 1) * seeds, :] = total
         send_mass(0)
+        acc[...] = jnp.zeros_like(acc)
         load_e.wait()
         for j in range(node_tiles):
             et[j] = jnp.transpose(et[j])
@@ -175,14 +184,36 @@
 
         def near(slot, blk, group):
             rows = slice(0, HALVES * seeds)
-            base = group * bufs
             for j in range(bufs):
-                c = base + j
-                stream_copy(c).wait()
+                c = group * bufs + j
+                turned_copy(c).wait()
                 lhs = left_side(slot, blk, range(HALVES), c % chunks // kts, j % kts)
                 for k in range(tiles):
-                    add(k, rows, product(lhs, stream[j, k], True), c == 0)
-                stream_copy((c + bufs) % (2 * chunks)).start()
+                    add(k, rows, product(lhs, stream[j, k], False), c == 0)
+                turned_copy((c + bufs) % (2 * chunks)).start()
+
+        def release(c):
+            turned_store(c).wait()
+            pl.when(c + bufs < 2 * chunks)(lambda: stream_copy(c + bufs).start())
+            pl.when(c + bufs >= 2 * chunks)(lambda: turned_copy(lax.rem(c + bufs, 2 * chunks)).start())
+
+        def near_first(slot, blk, base):
+            rows = slice(0, HALVES * seeds)
+
+            def trip(i, carry):
+                for j in range(bufs):
+                    c = base + i * bufs + j
+                    stream_copy(c).wait()
+                    lhs = left_side(slot, blk, range(HALVES), i * (bufs // kts) + j // kts, j % kts)
+                    for k in range(tiles):
+                        rhs = jnp.transpose(stream[j, k])
+                        stream[j, k] = rhs
+                        add(k, rows, product(lhs, rhs, False), False)
+                    pl.when(c >= 2)(lambda: release(c - 2))
+                    turned_store(c).start()
+                return carry
+
+            lax.fori_loop(0, chunks // bufs, trip, 0)
 
         def finish(t, slot, h):
             nxt = 1 - slot
@@ -250,19 +281,28 @@
                             arrive(slot, blocks[5], h, pair + j, 1, sib_r.at[slot, 4 + 2 * h + j])
                     compute(turn, slot, [(b, p) for p in range(pieces)], [h])
 
-            near(slot, me, 0)
-            if not first:
+            if first:
+                near_first(slot, me, 0)
+            else:
+                near(slot, me, 0)
                 wait_sends(1 - slot)
             pass_on(0, 0)
-            near(slot, me, 1)
+            if not first:
+                near(slot, me, 1)
             for h in both:
                 for u in range(2):
                     arrive(slot, sib, h, u * pair, pair, sib_own.at[slot, 2 * h + u])
-            near(slot, sib, 2)
+            if first:
+                near_first(slot, sib, chunks)
+            else:
+                near(slot, sib, 2)
             pass_on(0, 1)
-            near(slot, sib, 3)
             if first:
+                for c in (2 * chunks - 2, 2 * chunks - 1):
+                    release(c)
                 load_cache()
+            else:
+                near(slot, sib, 3)
             around(0, 1, [0], first)
             pass_on(1, 0)
             around(2, 1, [0], first)
@@ -296,7 +336,7 @@
 
         wait_sends((num_sweeps - 1) % 2)
         for c in range(bufs):
-            stream_copy(c).wait()
+            turned_copy(c).wait()
         for j in range(node_tiles):
             acc[j] = jnp.transpose(acc[j])
         store = pltpu.make_async_copy(acc, out3, io_sem.at[0])
@@ -320,11 +360,12 @@
         f32, bf16 = jnp.float32, jnp.bfloat16
         tile3 = (rows // lanes, lanes, num_seeds)
         dma, hbm = pltpu.SemaphoreType.DMA, pl.BlockSpec(memory_space=pl.ANY)
-        out = pl.pallas_call(
+        chunk3 = (2 * rows // TILE, tiles, TILE, TILE)
+        out, _ = pl.pallas_call(
             functools.partial(sweeps_kernel, n, damping.shape[0], num_nodes),
-            out_shape=jax.ShapeDtypeStruct(tile3, f32),
+            out_shape=(jax.ShapeDtypeStruct(tile3, f32), jax.ShapeDtypeStruct(chunk3, bf16)),
             in_specs=[pl.BlockSpec(memory_space=pltpu.VMEM), pl.BlockSpec(memory_space=pltpu.SMEM), hbm, hbm, hbm],
-            out_specs=hbm,
+            out_specs=(hbm, hbm),
             scratch_shapes=[
                 pltpu.VMEM(((n - 2) * pieces, width // TILE, tiles, TILE, TILE), bf16),
                 pltpu.VMEM((2, n, HALVES, pieces, num_seeds // HALVES, width), bf16),
@@ -336,7 +377,7 @@
                 pltpu.VMEM((num_seeds, lanes), f32),
                 dma((2, 8)), dma((2, 8)), dma((2, 4)), dma((2, 8)), dma((2, 8)),
                 dma((2,)), dma((2,)), dma((2,)),
-                dma(((n - 2) * pieces, width // TILE)), dma((bufs,)), dma((2,)),
+                dma(((n - 2) * pieces, width // TILE)), dma((bufs,)), dma((bufs,)), dma((2,)),
             ],
             compiler_params=pltpu.CompilerParams(collective_id=0, has_side_effects=True, vmem_limit_bytes=VMEM_LIMIT),
         )(

time: 366 us -> 364 us (level)
  no operation moved by 1% of the time
where the time goes in v4:
time: 364 us; the launch traced here: 363 us
  Pallas kernels  361 us (99%)
    pallas_call x1, Pallas kernels, local_sweeps(): pl.pallas_call(functools.partial(sweeps_kernel, n, damping.shape[0], num_...  361 us

profile of v4, /device:TPU:113, one launch (start us, length us, event | category | flops | bytes accessed | tf_op | source)
XLA Modules:
  0.0 363.1 jit_solution(2258257515811371334)
XLA Ops:
  0.0 360.8 %shard_map.55 = (f32[16,128,128]{2,1,0:T(8,128)}, bf16[16,8,256,256]{3,2,1,0:T(8,128)(2,1)}) custom-call(s32[16,128]{1,0:T(8,128)} %bitcast.8, f32[16]{0:T(128)} %damp.1, bf16[8,256,16384]{2,1,0:T(8,128)(2,1)} %bitcast.1.a3, f32[16,128,128]{2,1,0:T(8,128)} %bitcast.5, f32[16,128,128]{2,1,0:T(8,128)} %bitcast.6), custom_call_target="tpu_custom_call" | custom-call | tf_op jit(solution)/shard_map/pallas_call | solution.py:364
  360.8 2.3 copy.7

commit v5 on v2

--- a/solution.py
+++ b/solution.py
@@ -219,27 +219,34 @@
                 wait_sends(1 - slot)
 
             def pass_on(h, i):
-                arrive(slot, left, h, i * pair, pair, recv_l.at[slot, 2 * h + i])
-                if i == 0:
+                def far_right():
                     for j in range(pair):
                         send(slot, left, h, j, 1, recv_l.at[slot, 4 + 2 * h + j], right)
-                arrive(slot, right, h, (1 - i) * pair, pair, recv_r.at[slot, 2 * h + i])
-                if i == 0:
+
+                def far_left():
                     for j in range(pair):
                         send(slot, right, h, pair + j, 1, recv_r.at[slot, 4 + 2 * h + j], left)
+
+                arrive(slot, left, h, i * pair, pair, recv_l.at[slot, 2 * h + i])
+                pl.when(i == 0)(far_right)
+                arrive(slot, right, h, (1 - i) * pair, pair, recv_r.at[slot, 2 * h + i])
+                pl.when(i == 0)(far_left)
                 send(slot, left, h, i * pair, pair, sib_l.at[slot, 2 * h + i], sib)
                 send(slot, right, h, (1 - i) * pair, pair, sib_r.at[slot, 2 * h + i], sib)
 
             pass_on(0, 0)
             pass_on(0, 1)
-            for i in range(2):
+
+            def second(i, carry):
                 pass_on(1, i)
                 compute(first, slot, [(b, (i if b == 0 else 1 - i) * pair + j) for b in (0, 1) for j in range(pair)], range(HALVES))
                 for h in range(HALVES):
                     arrive(slot, blocks[2], h, i * pair, pair, sib_l.at[slot, 2 * h + i])
                     arrive(slot, blocks[3], h, (1 - i) * pair, pair, sib_r.at[slot, 2 * h + i])
                 compute(first, slot, [(b, (i if b == 2 else 1 - i) * pair + j) for b in (2, 3) for j in range(pair)], range(HALVES))
-
+                return carry
+
+            lax.fori_loop(0, 2, second, 0)
             wait_mass(slot)
             row = jnp.sum(pm[slot], axis=0)[0:1]
             mcol[...] = jnp.transpose(jnp.broadcast_to(row, (lanes, HALVES * seeds)))

time: 351 us -> 355 us (1.011)
  no operation moved by 1% of the time
where the time goes in v5:
time: 355 us; the launch traced here: 354 us
  Pallas kernels  352 us (99%)
    pallas_call x1, Pallas kernels, local_sweeps(): pl.pallas_call(functools.partial(sweeps_kernel, n, damping.shape[0], num_...  352 us

profile of v5, /device:TPU:113, one launch (start us, length us, event | category | flops | bytes accessed | tf_op | source)
XLA Modules:
  0.0 354.2 jit_solution(16667853781598586324)
XLA Ops:
  0.0 351.9 %shard_map.55 = f32[16,128,128]{2,1,0:T(8,128)} custom-call(s32[16,128]{1,0:T(8,128)} %bitcast.8, f32[16]{0:T(128)} %damp.1, bf16[8,256,16384]{2,1,0:T(8,128)(2,1)} %bitcast.1.a3, f32[16,128,128]{2,1,0:T(8,128)} %bitcast.6, f32[16,128,128]{2,1,0:T(8,128)} %bitcast.7), custom_call_target="tpu_custom_call" | custom-call | tf_op jit(solution)/shard_map/pallas_call | solution.py:311
  351.9 2.3 copy.7
